TPU v7x, 32 devices: a whole 2x2x4 slice. The times are simulated.
32 devices in a mesh: bra: 8 (over z, x), ket: 2 (over y), mpo: 2 (over core).
Axes of the slice: x: 2, y: 2, z: 4, core: 2. Of those that a mesh axis runs over, the one named last changes fastest.
Arguments:
- left_env: bfloat16 [4, 3072, 3072], P('mpo', 'bra', 'ket'), may hold values from -6 to 6
- site_tensor: bfloat16 [3072, 4, 3072], P('bra', None, 'ket'), may hold values from -0.0546875 to 0.0546875
- block_values: float32 [12, 4, 4], replicated, may hold values from -3 to 3
- pair_in: int32 [12], replicated, may hold values from 0 to 3
- pair_out: int32 [12], replicated, may hold values from 0 to 3, as said below
Outputs:
- new_env: bfloat16 [4, 3072, 3072], P('mpo', 'bra', 'ket')
Inputs may be any that keep to these rules, and one draw needn't show every extreme that they name: `pair_out`: every component number 0 to 3 appears at least once.
All inputs are finite; a program needn't handle non-finite values.
Results may differ from a plain program's by a relative error of at most 0.018.
Values may be sent and summed in bfloat16 or wider, within the bound.
A program may use at most 192 MiB of HBM per device.

v0:
```python
import jax
import jax.numpy as jnp
from jax import lax
from jax.sharding import PartitionSpec as P

K = 4


def local(left_env, site_tensor, block_values, pair_in, pair_out):
    comps_loc = left_env.shape[0]
    rows_loc = left_env.shape[1]
    cols_loc = left_env.shape[2]
    phys = site_tensor.shape[1]
    comps = jnp.arange(K, dtype=jnp.int32)
    hot_out = (pair_out[:, None] == comps[None, :]).astype(jnp.float32)
    hot_in = (pair_in[:, None] == comps[None, :]).astype(jnp.float32)
    mixing = jnp.einsum(
        "pv,pw,pst->vswt", hot_out, hot_in, block_values, precision=lax.Precision.HIGHEST
    )
    splits = lax.axis_size("mpo")
    half_cols = cols_loc // splits
    own_start = lax.axis_index("mpo") * half_cols
    site_own = lax.dynamic_slice_in_dim(site_tensor, own_start, half_cols, 2)
    site_full = lax.all_gather(
        site_own.reshape(rows_loc, phys * half_cols), "bra", axis=0, tiled=True
    )
    piece = lax.all_gather(left_env, "ket", axis=2, tiled=True)
    piece = lax.all_gather(piece, "mpo", axis=0, tiled=True)
    comps_all, width = (piece.shape[0], piece.shape[2])
    half = jnp.dot(
        piece.reshape(comps_all * rows_loc, width), site_full, preferred_element_type=jnp.float32
    )
    half = half.astype(jnp.bfloat16).reshape(comps_all, rows_loc, phys, half_cols)
    mixed = jnp.einsum(
        "vswt,watc->savc", mixing, half.astype(jnp.float32), precision=lax.Precision.HIGHEST
    ).astype(jnp.bfloat16)
    mixed_pairs = mixed.reshape(phys * rows_loc, comps_all * half_cols)
    site_wide = lax.all_gather(jnp.transpose(site_tensor, (1, 0, 2)), "ket", axis=2, tiled=True)
    site_pairs = site_wide.reshape(phys * rows_loc, site_wide.shape[2])
    term = lax.dot_general(
        site_pairs, mixed_pairs, (((0,), (0,)), ((), ())), preferred_element_type=jnp.float32
    ).astype(jnp.bfloat16)
    owned = lax.psum_scatter(term, "bra", scatter_dimension=0, tiled=True)
    owned = jnp.transpose(owned.reshape(-1, comps_all, half_cols), (1, 0, 2))
    return lax.all_to_all(owned, "mpo", split_axis=0, concat_axis=2, tiled=True)


def solution(mesh):
    return jax.shard_map(
        local,
        mesh=mesh,
        in_specs=(P("mpo", "bra", "ket"), P("bra", None, "ket"), P(), P(), P()),
        out_specs=P("mpo", "bra", "ket"),
        check_vma=False,
    )
```

profile of v0, /device:TPU:0, one launch (start us, length us, event | category | flops | bytes accessed | tf_op | source)
XLA Modules:
  0.0 978.1 jit_solution(10487822228750793544)
XLA Ops:
  6.5 0.7 all-gather.7.cloned.1.call-update
  7.3 0.0 all-gather.9.cloned.1.call-start
  7.3 67.0 %all-gather.7.cloned.1.call-done = bf16[2,384,3072]{2,1,0:T(8,128)(2,1)} async-done(((bf16[2,384,1536]{2,1,0:T(8,128)(2,1)}), bf16[2,384,3072]{2,1,0:T(8,128)(2,1)}) %all-gather.7.cloned.1.call-update) | async-done | bytes 4718608 | tf_op jit(solution)/shard_map/all_gather | solution.py:27
  74.3 0.0 all-gather.9.cloned.1.call-update
  74.3 0.0 all-gather.5.cloned.1.call-start
  74.3 2.5 constant_dynamic-slice_fusion
  76.8 1.9 copy.27
  78.7 0.0 all-gather.5.cloned.1.call-update
  78.7 0.0 all-gather.11.cloned.1.call-start
  78.8 5.8 copy.34
  84.5 0.0 all-gather.11.cloned.1.call-update
  84.6 0.0 reduce-scatter.4.cloned.1.call-start
  84.6 0.0 copy-done.1
  84.6 0.0 copy-done.2
  84.7 0.3 convolution_bitcast_fusion
  85.0 12.5 %all-gather.9.cloned.1.call-done = bf16[4,384,3072]{2,1,0:T(8,128)(2,1)} async-done(((bf16[2,384,3072]{2,1,0:T(8,128)(2,1)}), bf16[4,384,3072]{2,1,0:T(8,128)(2,1)}) %all-gather.9.cloned.1.call-update) | async-done | bytes 9437200 | tf_op jit(solution)/shard_map/all_gather | solution.py:28
  97.5 365.1 %all-gather.5.cloned.1.call-done = bf16[3072,3072]{1,0:T(8,128)(2,1)} async-done(((bf16[384,3072]{1,0:T(8,128)(2,1)}), bf16[3072,3072]{1,0:T(8,128)(2,1)}) %all-gather.5.cloned.1.call-update) | async-done | bytes 18874384 | tf_op jit(solution)/shard_map/all_gather | solution.py:24
  462.6 36.7 %fusion = bf16[1536,3072]{0,1:T(8,128)(2,1)} fusion(bf16[3072,3072]{1,0:T(8,128)(2,1)} %all-gather.5.cloned.1.call-done, bf16[1536,3072]{1,0:T(8,128)(2,1)} %bitcast.57), kind=kOutput, calls=%fused_computation.3 | convolution fusion | flops 28995747840 | bytes 37748736 | tf_op jit(solution)/shard_map/dot_general | solution.py:30
  499.3 16.5 %reshape.22 = bf16[4,384,4,768]{1,0,3,2:T(4,128)(2,1)} reshape(bf16[1536,3072]{0,1:T(8,128)(2,1)} %fusion) | data formatting | bytes 18874368 | tf_op jit(solution)/shard_map/reshape | solution.py:33
  515.8 19.3 %copy.19 = bf16[4,384,4,768,1]{3,0,2,4,1:T(4,128)(2,1)} copy(bf16[4,384,4,768,1]{1,0,3,2,4:T(4,128)(2,1)} %bitcast.48) | data formatting | bytes 18874368 | tf_op jit(solution)/shard_map/reshape | solution.py:33
  535.0 20.1 %fusion.1 = bf16[4,384,4,768]{3,0,2,1:T(4,128)(2,1)S(1)} fusion(bf16[4,384,4,768,1]{3,0,2,4,1:T(4,128)(2,1)} %copy.19, f32[4,4,4,4,1]{1,2,3,0,4:T(4,128)S(1)} %convolution_bitcast_fusion), kind=kOutput, calls=%fused_computation.4 | convolution fusion | flops 910688256 | bytes 18875392 | tf_op jit(solution)/shard_map/vswt,watc->savc/dot_general | solution.py:34
  555.2 6.2 copy.15
  561.4 9.6 copy.28
  571.0 11.0 %all-gather.11.cloned.1.call-done = bf16[4,384,3072]{2,1,0:T(8,128)(2,1)} async-done(((bf16[4,384,1536]{2,1,0:T(8,128)(2,1)}), bf16[4,384,3072]{2,1,0:T(8,128)(2,1)}) %all-gather.11.cloned.1.call-update) | async-done | bytes 9437200 | tf_op jit(solution)/shard_map/all_gather | solution.py:38
  582.0 36.8 %convert_bitcast_fusion = bf16[3072,3072]{0,1:T(8,128)(2,1)} fusion(bf16[1536,3072]{1,0:T(8,128)(2,1)} %bitcast.51, bf16[1536,3072]{1,0:T(8,128)(2,1)} %bitcast.58), kind=kOutput, calls=%fused_computation.1 | convolution fusion | flops 29000466432 | bytes 37748736 | tf_op jit(solution)/shard_map/dot_general | solution.py:40
  618.8 24.6 %copy.25 = bf16[3072,3072]{1,0:T(8,128)(2,1)} copy(bf16[3072,3072]{0,1:T(8,128)(2,1)} %convert_bitcast_fusion) | data formatting | bytes 37748736
  643.4 0.0 reduce-scatter.4.cloned.1.call-update
  643.4 309.9 %reduce-scatter.4.cloned.1.call-done = bf16[384,3072]{1,0:T(8,128)(2,1)} async-done(((bf16[3072,3072]{1,0:T(8,128)(2,1)}), bf16[384,3072]{1,0:T(8,128)(2,1)}) %reduce-scatter.4.cloned.1.call-update) | async-done | bytes 2359312
  953.3 3.0 copy.26
  956.3 6.5 all_to_all.18
  962.9 6.0 copy.17
  968.8 2.8 all_to_all.16
  (6 shorter events, 0.0 us)
Async XLA Ops:
  6.5 67.7 %all-gather.7.cloned.1.call-start = ((), (), s32[]{:S(2)}) async-start(), calls=%async_computation.3 | async-start | bytes 7077888 | tf_op jit(solution)/shard_map/all_gather | solution.py:27
  7.3 90.2 %all-gather.9.cloned.1.call-start = ((), (), s32[]{:S(2)}) async-start(), calls=%async_computation.4 | async-start | bytes 14155776 | tf_op jit(solution)/shard_map/all_gather | solution.py:28
  74.3 388.3 %all-gather.5.cloned.1.call-start = ((), (), s32[]{:S(2)}) async-start(), calls=%async_computation.2 | async-start | bytes 21233664 | tf_op jit(solution)/shard_map/all_gather | solution.py:24
  78.7 5.9 copy-start.1
  78.7 5.9 copy-start.2
  78.7 5.9 copy-start
  78.7 503.3 %all-gather.11.cloned.1.call-start = ((), (), s32[]{:S(2)}) async-start(), calls=%async_computation.5 | async-start | bytes 14155776 | tf_op jit(solution)/shard_map/all_gather | solution.py:38
  84.6 868.7 %reduce-scatter.4.cloned.1.call-start = ((), (), s32[]{:S(2)}) async-start(), calls=%async_computation.6 | async-start | bytes 21233664
Sparse Core Ops, SparseCore 0:
  8.9 65.3 all-gather.6
  75.8 21.6 all-gather.8
  99.0 363.5 all-gather.4
  464.0 117.9 all-gather.10
  643.5 309.7 reduce-scatter.3
where the time goes:
time: 980 us; the launch traced here: 978 us
  waiting for transfers between devices  766 us (78%)
  local copies, waits for them, and re-layouts  98 us (10%)
  matrix products  93.9 us (10%)
  between operations  13.2 us (1%)
    all_gather x1, waiting for transfers between devices, local(): lax.all_gather(site_own.reshape(rows_loc, phys * half_cols), 'bra', axis=...  365 us
    unnamed x6, waiting for transfers between devices  311 us
    all_gather x1, waiting for transfers between devices, local(): piece = lax.all_gather(left_env, 'ket', axis=2, tiled=True)  67 us
    unnamed x11, local copies, waits for them, and re-layouts  44.8 us
    dot_general x1, matrix products, local(): lax.dot_general(site_pairs, mixed_pairs, (((0,), (0,)), ((), ())), prefer...  36.8 us
    dot_general x1, matrix products, local(): jnp.dot(piece.reshape(comps_all * rows_loc, width), site_full, preferred_...  36.7 us
    reshape x2, local copies, waits for them, and re-layouts, local(): half.astype(jnp.bfloat16).reshape(comps_all, rows_loc, phys, half_cols)  35.7 us
    dot_general x1, matrix products, local(): jnp.einsum('vswt,watc->savc', mixing, half.astype(jnp.float32), precision...  20.1 us
  transfers between devices with their start and end apart: 5, of which 5 were waited for; matrix products, arithmetic and copies ran while one was open for 12% of the time, Pallas kernels for 0%

commit v1 on v0

--- a/solution.py
+++ b/solution.py
@@ -4,6 +4,23 @@
 from jax.sharding import PartitionSpec as P
 
 K = 4
+
+
+def joined_along(tiles, dim):
+    shape = list(tiles.shape[1:])
+    shape[dim] *= tiles.shape[0]
+    return jnp.moveaxis(tiles, 0, dim).reshape(shape)
+
+
+def ring_gather(x, axis, dim):
+    size = lax.axis_size(axis)
+    forward = [(i, (i + 1) % size) for i in range(size)]
+    parts = [x]
+    while len(parts) < size:
+        parts.append(lax.ppermute(parts[-1], axis, forward))
+    place = lax.axis_index(axis)
+    parts = jnp.stack(parts)[(place - jnp.arange(size)) % size]
+    return joined_along(parts, dim)
 
 
 def local(left_env, site_tensor, block_values, pair_in, pair_out):
@@ -21,9 +38,7 @@
     half_cols = cols_loc // splits
     own_start = lax.axis_index("mpo") * half_cols
     site_own = lax.dynamic_slice_in_dim(site_tensor, own_start, half_cols, 2)
-    site_full = lax.all_gather(
-        site_own.reshape(rows_loc, phys * half_cols), "bra", axis=0, tiled=True
-    )
+    site_full = ring_gather(site_own.reshape(rows_loc, phys * half_cols), "bra", 0)
     piece = lax.all_gather(left_env, "ket", axis=2, tiled=True)
     piece = lax.all_gather(piece, "mpo", axis=0, tiled=True)
     comps_all, width = (piece.shape[0], piece.shape[2])

time: 980 us -> 943 us (0.962)
  waiting for transfers between devices: 766 us -> 670 us
  local copies, waits for them, and re-layouts: 98 us -> 136 us
  other arithmetic: 0.01 us -> 16.2 us
    all_gather x1 -> x0, waiting for transfers between devices: 365 us -> none  [local(): lax.all_gather(site_own.reshape(rows_loc, phys * half_cols), 'bra', axis=...]
    ppermute x0 -> x7, waiting for transfers between devices: none -> 303 us  [ring_gather(): parts.append(lax.ppermute(parts[-1], axis, forward))]
    gather x0 -> x3, local copies, waits for them, and re-layouts: none -> 24.4 us  [ring_gather(): parts = jnp.stack(parts)[(place - jnp.arange(size)) % size]]
    unnamed x0 -> x1, other arithmetic: none -> 16.1 us
    all_gather x1, waiting for transfers between devices: 12.5 us -> 0.01 us  [local(): piece = lax.all_gather(piece, 'mpo', axis=0, tiled=True)]
    all_gather x1, waiting for transfers between devices: 11 us -> 0.01 us  [local(): lax.all_gather(jnp.transpose(site_tensor, (1, 0, 2)), 'ket', axis=2, tile...]
    unnamed x11 -> x26, local copies, waits for them, and re-layouts: 44.8 us -> 55.3 us
    unnamed x6 -> x5, waiting for transfers between devices: 311 us -> 308 us
  transfers between devices with their start and end apart: 5 -> 11, of which waited for: 5 -> 8; matrix products, arithmetic and copies ran while one was open for 12% -> 18% of each run, Pallas kernels for 0% -> 0%
where the time goes in v1:
time: 943 us; the launch traced here: 941 us
  waiting for transfers between devices  670 us (71%)
  local copies, waits for them, and re-layouts  136 us (14%)
  matrix products  93.9 us (10%)
  other arithmetic  16.2 us (2%)
  between operations  13.3 us (1%)
    unnamed x5, waiting for transfers between devices  308 us
    ppermute x7, waiting for transfers between devices, ring_gather(): parts.append(lax.ppermute(parts[-1], axis, forward))  303 us
    all_gather x1, waiting for transfers between devices, local(): piece = lax.all_gather(left_env, 'ket', axis=2, tiled=True)  59.6 us
    unnamed x26, local copies, waits for them, and re-layouts  55.3 us
    dot_general x1, matrix products, local(): lax.dot_general(site_pairs, mixed_pairs, (((0,), (0,)), ((), ())), prefer...  36.8 us
    dot_general x1, matrix products, local(): jnp.dot(piece.reshape(comps_all * rows_loc, width), site_full, preferred_...  36.7 us
    reshape x2, local copies, waits for them, and re-layouts, local(): half.astype(jnp.bfloat16).reshape(comps_all, rows_loc, phys, half_cols)  35.7 us
    gather x3, local copies, waits for them, and re-layouts, ring_gather(): parts = jnp.stack(parts)[(place - jnp.arange(size)) % size]  24.4 us
  transfers between devices with their start and end apart: 11, of which 8 were waited for; matrix products, arithmetic and copies ran while one was open for 18% of the time, Pallas kernels for 0%

profile of v1, /device:TPU:0, one launch (start us, length us, event | category | flops | bytes accessed | tf_op | source)
XLA Modules:
  0.0 940.8 jit_solution(12870490741794794804)
XLA Ops:
  7.3 2.5 constant_dynamic-slice_fusion
  9.8 1.9 copy.27
  11.7 3.0 collective-permute-start
  14.6 59.6 %all-gather.4.cloned.1.call-done = bf16[2,384,3072]{2,1,0:T(8,128)(2,1)} async-done(((bf16[2,384,1536]{2,1,0:T(8,128)(2,1)}), bf16[2,384,3072]{2,1,0:T(8,128)(2,1)}) %all-gather.4.cloned.1.call-update) | async-done | bytes 4718608 | tf_op jit(solution)/shard_map/all_gather | solution.py:42
  75.9 54.3 %collective-permute-done.1 = bf16[384,3072]{1,0:T(8,128)(2,1)S(1)} collective-permute-done((bf16[384,3072]{1,0:T(8,128)(2,1)}, bf16[384,3072]{1,0:T(8,128)(2,1)S(1)}, u32[]{:S(2)}, u32[]{:S(2)}) %collective-permute-start.1) | collective-permute-done | bytes 2359328 | tf_op jit(solution)/shard_map/ppermute | solution.py:20
  131.6 54.7 %collective-permute-done.2 = bf16[384,3072]{1,0:T(8,128)(2,1)S(1)} collective-permute-done((bf16[384,3072]{1,0:T(8,128)(2,1)S(1)}, bf16[384,3072]{1,0:T(8,128)(2,1)S(1)}, u32[]{:S(2)}, u32[]{:S(2)}) %collective-permute-start.2) | collective-permute-done | bytes 2359328 | tf_op jit(solution)/shard_map/ppermute | solution.py:20
  187.7 53.9 %collective-permute-done.3 = bf16[384,3072]{1,0:T(8,128)(2,1)} collective-permute-done((bf16[384,3072]{1,0:T(8,128)(2,1)S(1)}, bf16[384,3072]{1,0:T(8,128)(2,1)}, u32[]{:S(2)}, u32[]{:S(2)}) %collective-permute-start.3) | collective-permute-done | bytes 2359328 | tf_op jit(solution)/shard_map/ppermute | solution.py:20
  241.6 5.4 copy.34
  247.1 2.9 stack_reshape.3
  250.4 2.0 constant_dynamic-update-slice_fusion
  252.4 42.4 %collective-permute-done.4 = bf16[384,3072]{1,0:T(8,128)(2,1)} collective-permute-done((bf16[384,3072]{1,0:T(8,128)(2,1)}, bf16[384,3072]{1,0:T(8,128)(2,1)}, u32[]{:S(2)}, u32[]{:S(2)}) %collective-permute-start.4) | collective-permute-done | bytes 2359328 | tf_op jit(solution)/shard_map/ppermute | solution.py:20
  294.9 1.8 bitcast_dynamic-update-slice_fusion.6
  297.1 50.1 %collective-permute-done.5 = bf16[384,3072]{1,0:T(8,128)(2,1)S(1)} collective-permute-done((bf16[384,3072]{1,0:T(8,128)(2,1)}, bf16[384,3072]{1,0:T(8,128)(2,1)S(1)}, u32[]{:S(2)}, u32[]{:S(2)}) %collective-permute-start.5) | collective-permute-done | bytes 2359328 | tf_op jit(solution)/shard_map/ppermute | solution.py:20
  349.0 1.8 bitcast_dynamic-update-slice_fusion.2
  351.0 47.4 %collective-permute-done.6 = bf16[384,3072]{1,0:T(8,128)(2,1)S(1)} collective-permute-done((bf16[384,3072]{1,0:T(8,128)(2,1)S(1)}, bf16[384,3072]{1,0:T(8,128)(2,1)S(1)}, u32[]{:S(2)}, u32[]{:S(2)}) %collective-permute-start.6) | collective-permute-done | bytes 2359328 | tf_op jit(solution)/shard_map/ppermute | solution.py:20
  398.6 6.8 fusion.12
  405.4 8.9 gather_fusion
  414.2 8.8 gather_fusion.1
  423.0 16.1 %pad_maximum_fusion = bf16[8,384,3072]{2,1,0:T(8,128)(2,1)} fusion(bf16[8,384,1536]{2,1,0:T(8,128)(2,1)} %gather_fusion.1, bf16[8,384,1536]{2,1,0:T(8,128)(2,1)} %gather_fusion), kind=kLoop, calls=%fused_computation.2 | loop fusion | flops 37748736 | bytes 37748736
  439.2 36.7 %fusion = bf16[1536,3072]{0,1:T(8,128)(2,1)} fusion(bf16[3072,3072]{1,0:T(8,128)(2,1)} %bitcast.68, bf16[1536,3072]{1,0:T(8,128)(2,1)} %bitcast.74), kind=kOutput, calls=%fused_computation.6 | convolution fusion | flops 28995747840 | bytes 37748736 | tf_op jit(solution)/shard_map/dot_general | solution.py:45
  475.9 16.4 %reshape.75 = bf16[4,384,4,768]{1,0,3,2:T(4,128)(2,1)} reshape(bf16[1536,3072]{0,1:T(8,128)(2,1)} %fusion) | data formatting | bytes 18874368 | tf_op jit(solution)/shard_map/reshape | solution.py:48
  492.3 19.2 %copy.19 = bf16[4,384,4,768,1]{3,0,2,4,1:T(4,128)(2,1)} copy(bf16[4,384,4,768,1]{1,0,3,2,4:T(4,128)(2,1)} %bitcast.65) | data formatting | bytes 18874368 | tf_op jit(solution)/shard_map/reshape | solution.py:48
  511.5 20.1 %fusion.1 = bf16[4,384,4,768]{3,0,2,1:T(4,128)(2,1)S(1)} fusion(bf16[4,384,4,768,1]{3,0,2,4,1:T(4,128)(2,1)} %copy.19, f32[4,4,4,4,1]{1,2,3,0,4:T(4,128)S(1)} %convolution_bitcast_fusion), kind=kOutput, calls=%fused_computation.7 | convolution fusion | flops 910688256 | bytes 18875392 | tf_op jit(solution)/shard_map/vswt,watc->savc/dot_general | solution.py:49
  531.7 6.2 copy.15
  537.9 9.6 %copy.28 = bf16[192,8,4,768]{3,1,2,0:T(8,128)(2,1)} copy(bf16[192,8,4,768]{3,2,1,0:T(4,128)(2,1)} %bitcast.66) | data formatting | bytes 18874368
  547.5 36.8 %convert_bitcast_fusion = bf16[3072,3072]{0,1:T(8,128)(2,1)} fusion(bf16[1536,3072]{1,0:T(8,128)(2,1)} %bitcast.70, bf16[1536,3072]{1,0:T(8,128)(2,1)} %bitcast.75), kind=kOutput, calls=%fused_computation.4 | convolution fusion | flops 29000466432 | bytes 37748736 | tf_op jit(solution)/shard_map/dot_general | solution.py:55
  584.3 24.7 %copy.25 = bf16[3072,3072]{1,0:T(8,128)(2,1)} copy(bf16[3072,3072]{0,1:T(8,128)(2,1)} %convert_bitcast_fusion) | data formatting | bytes 37748736
  608.9 307.0 %reduce-scatter.4.cloned.1.call-done = bf16[384,3072]{1,0:T(8,128)(2,1)} async-done(((bf16[3072,3072]{1,0:T(8,128)(2,1)}), bf16[384,3072]{1,0:T(8,128)(2,1)}) %reduce-scatter.4.cloned.1.call-update) | async-done | bytes 2359312
  916.0 3.0 copy.26
  919.0 6.6 all_to_all.18
  925.5 6.0 copy.17
  931.5 2.8 all_to_all.16
  (40 shorter events, 8.1 us)
Async XLA Ops:
  6.5 67.7 %all-gather.4.cloned.1.call-start = ((), (), s32[]{:S(2)}) async-start(), calls=%async_computation.2 | async-start | bytes 7077888 | tf_op jit(solution)/shard_map/all_gather | solution.py:42
  7.3 431.9 %all-gather.6.cloned.1.call-start = ((), (), s32[]{:S(2)}) async-start(), calls=%async_computation.3 | async-start | bytes 14155776 | tf_op jit(solution)/shard_map/all_gather | solution.py:43
  11.7 62.7 %collective-permute-start = (bf16[384,3072]{1,0:T(8,128)(2,1)}, bf16[384,3072]{1,0:T(8,128)(2,1)}, u32[]{:S(2)}, u32[]{:S(2)}) collective-permute-start(bf16[384,3072]{1,0:T(8,128)(2,1)} %bitcast.32), channel_id=1, source_target_pairs={{0,4},{4,8},{8,12},{12,16},{16,20},{20,24},{24,28},{28,0},{1,5},{5... | collective-permute-start | bytes 7077896 | tf_op jit(solution)/shard_map/ppermute | solution.py:20
  74.3 175.7 %copy-start.5 = (s32[12]{0:T(128)S(1)}, s32[12]{0:T(128)}, u32[]{:S(2)}) copy-start(s32[12]{0:T(128)} %param.8) | copy-start | bytes 148
  74.3 175.7 %copy-start.6 = (s32[12]{0:T(128)S(1)}, s32[12]{0:T(128)}, u32[]{:S(2)}) copy-start(s32[12]{0:T(128)} %param.9) | copy-start | bytes 148
  74.3 175.8 %copy-start.4 = (f32[12,4,4]{0,2,1:T(4,128)S(1)}, f32[12,4,4]{0,2,1:T(4,128)}, u32[]{:S(2)}) copy-start(f32[12,4,4]{0,2,1:T(4,128)} %param.7) | copy-start | bytes 2308
  74.3 473.2 %all-gather.8.cloned.1.call-start = ((), (), s32[]{:S(2)}) async-start(), calls=%async_computation.4 | async-start | bytes 14155776 | tf_op jit(solution)/shard_map/all_gather | solution.py:53
  74.4 55.8 %collective-permute-start.1 = (bf16[384,3072]{1,0:T(8,128)(2,1)}, bf16[384,3072]{1,0:T(8,128)(2,1)S(1)}, u32[]{:S(2)}, u32[]{:S(2)}) collective-permute-start(bf16[384,3072]{1,0:T(8,128)(2,1)} %collective-permute-done), channel_id=1, source_target_pairs={{0,4},{4,8},{8,12},{12,16},{16,20},{20,24},{24,28},{28,0},{1,5},{5... | collective-permute-start | bytes 7077896 | tf_op jit(solution)/shard_map/ppermute | solution.py:20
  130.2 1.4 copy-start
  131.6 54.7 %collective-permute-start.2 = (bf16[384,3072]{1,0:T(8,128)(2,1)S(1)}, bf16[384,3072]{1,0:T(8,128)(2,1)S(1)}, u32[]{:S(2)}, u32[]{:S(2)}) collective-permute-start(bf16[384,3072]{1,0:T(8,128)(2,1)S(1)} %collective-permute-done.1), channel_id=1, source_target_pairs={{0,4},{4,8},{8,12},{12,16},{16,20},{20,24},{24,28},{28,0},{1,5},{5... | collective-permute-start | bytes 7077896 | tf_op jit(solution)/shard_map/ppermute | solution.py:20
  186.3 1.4 copy-start.2
  187.7 53.9 %collective-permute-start.3 = (bf16[384,3072]{1,0:T(8,128)(2,1)S(1)}, bf16[384,3072]{1,0:T(8,128)(2,1)}, u32[]{:S(2)}, u32[]{:S(2)}) collective-permute-start(bf16[384,3072]{1,0:T(8,128)(2,1)S(1)} %collective-permute-done.2), channel_id=1, source_target_pairs={{0,4},{4,8},{8,12},{12,16},{16,20},{20,24},{24,28},{28,0},{1,5},{5... | collective-permute-start | bytes 7077896 | tf_op jit(solution)/shard_map/ppermute | solution.py:20
  241.6 53.3 %collective-permute-start.4 = (bf16[384,3072]{1,0:T(8,128)(2,1)}, bf16[384,3072]{1,0:T(8,128)(2,1)}, u32[]{:S(2)}, u32[]{:S(2)}) collective-permute-start(bf16[384,3072]{1,0:T(8,128)(2,1)} %collective-permute-done.3), channel_id=1, source_target_pairs={{0,4},{4,8},{8,12},{12,16},{16,20},{20,24},{24,28},{28,0},{1,5},{5... | collective-permute-start | bytes 7077896 | tf_op jit(solution)/shard_map/ppermute | solution.py:20
  247.0 669.0 %reduce-scatter.4.cloned.1.call-start = ((), (), s32[]{:S(2)}) async-start(), calls=%async_computation.5 | async-start | bytes 21233664
  250.0 46.7 %copy-start.1 = (bf16[384,3072]{1,0:T(8,128)(2,1)S(1)}, bf16[384,3072]{1,0:T(8,128)(2,1)}, u32[]{:S(2)}) copy-start(bf16[384,3072]{1,0:T(8,128)(2,1)} %copy-done) | copy-start | bytes 7077892
  250.0 46.9 %copy-start.3 = (bf16[384,3072]{1,0:T(8,128)(2,1)S(1)}, bf16[384,3072]{1,0:T(8,128)(2,1)}, u32[]{:S(2)}) copy-start(bf16[384,3072]{1,0:T(8,128)(2,1)} %copy-done.2) | copy-start | bytes 7077892
  294.9 52.3 %collective-permute-start.5 = (bf16[384,3072]{1,0:T(8,128)(2,1)}, bf16[384,3072]{1,0:T(8,128)(2,1)S(1)}, u32[]{:S(2)}, u32[]{:S(2)}) collective-permute-start(bf16[384,3072]{1,0:T(8,128)(2,1)} %collective-permute-done.4), channel_id=1, source_target_pairs={{0,4},{4,8},{8,12},{12,16},{16,20},{20,24},{24,28},{28,0},{1,5},{5... | collective-permute-start | bytes 7077896 | tf_op jit(solution)/shard_map/ppermute | solution.py:20
  347.2 51.2 %collective-permute-start.6 = (bf16[384,3072]{1,0:T(8,128)(2,1)S(1)}, bf16[384,3072]{1,0:T(8,128)(2,1)S(1)}, u32[]{:S(2)}, u32[]{:S(2)}) collective-permute-start(bf16[384,3072]{1,0:T(8,128)(2,1)S(1)} %collective-permute-done.5), channel_id=1, source_target_pairs={{0,4},{4,8},{8,12},{12,16},{16,20},{20,24},{24,28},{28,0},{1,5},{5... | collective-permute-start | bytes 7077896 | tf_op jit(solution)/shard_map/ppermute | solution.py:20
Sparse Core Ops, SparseCore 0:
  8.9 65.3 all-gather.3
  75.8 21.6 all-gather.5
  247.1 118.7 all-gather.7
  609.1 306.8 reduce-scatter.3
